TPU v7x, 128 devices: a whole 4x4x4 slice. The times are simulated.
128 devices in a mesh: book: 8 (over y, core), path: 16 (over z, x).
Axes of the slice: x: 4, y: 4, z: 4, core: 2. Of those that a mesh axis runs over, the one named last changes fastest.
Arguments:
- states: float32 [10, 20, 262144], P(None, None, ('book', 'path')), parts along dimension 2, may hold values from -7.5 to 7.5
- itm_flags: int32 [10, 262144], P(None, ('book', 'path')), parts along dimension 1, may hold values 0 or 1
- terminal: float32 [262144], P(('book', 'path')), parts along dimension 0, may hold values from -3.5 to 5.5
- strike: float32 [8], P('book'), parts along dimension 0, may hold values from 0.025 to 0.035
- date_index: int32 [262144], P(('book', 'path')), parts along dimension 0, may hold values from 0 to 9
Outputs:
- cash_flow: float32 [262144], P(('book', 'path')), parts along dimension 0
- book_price: float32 [8], P('book'), parts along dimension 0
- coefficients: float32 [80, 231], P('book'), parts along dimension 0
There are 8 independent parts, one for each index of `book`. A program takes and returns all parts, laid end to end along the dimension named above; each array names one. Nothing has to cross between parts.
All inputs are finite; a program needn't handle non-finite values. No bound on the sum of `itm_flags` on one device may be relied on, other than what follows from the above.
Results may differ from a plain program's by a relative error of at most 0.0003.
Values sent between devices are 32-bit elements; how exact they have to be, the bound alone decides.
A program may use at most 192 MiB of HBM per device.

v0:
```python
import jax
import jax.numpy as jnp
import numpy as np
from jax import lax
from jax.sharding import Mesh
from jax.sharding import PartitionSpec as P

PATH = ("path_0", "path_1")
BOOK_PATH = ("book", "path_0", "path_1")
ridge_weight = 0.05
temper_scale = 0.5
highest = lax.Precision.HIGHEST


def one_axis_at_a_time(shard, axes):
    for axis in axes:
        shard = lax.psum(shard, axis)
    return shard


def sent_to_all(shard, axis):
    length = lax.axis_size(axis)
    return lax.all_to_all(
        jnp.broadcast_to(shard[None], (length, *shard.shape)), axis, 0, 0, tiled=True
    )


def over_copies(shard, axis):
    return sent_to_all(shard, axis).sum(axis=0)


def swap_terms(factors, strike_level):
    forwards = 0.03 * jnp.exp(0.25 * factors)
    discount = jnp.cumprod(1.0 / (1.0 + 0.25 * forwards), axis=0)
    annuity = 0.25 * jnp.sum(discount, axis=0)
    swap_rate = (1.0 - discount[-1]) / annuity
    return (100.0 * annuity * (swap_rate - strike_level), discount[0])


def basis_of(scaled, pair_left, pair_right):
    ones_row = jnp.ones((1, scaled.shape[1]), jnp.float32)
    return jnp.concatenate([ones_row, scaled, scaled[pair_left] * scaled[pair_right]], axis=0)


def gram_only(basis_rows, money_flags):
    weighted = basis_rows * money_flags
    return lax.dot_general(
        weighted,
        basis_rows,
        (((1,), (1,)), ((), ())),
        precision=highest,
        preferred_element_type=jnp.float32,
    )


def system_of(gram_sums, path_count):
    return gram_sums / path_count + ridge_weight * jnp.eye(gram_sums.shape[0], dtype=jnp.float32)


def shards(states, itm_flags, terminal, strike, date_index):
    date_count, factor_count, local_paths = states.shape
    pair_left, pair_right = np.triu_indices(factor_count)
    total_paths = local_paths * lax.axis_size(PATH)
    value_now = terminal
    coef_list = []
    money_all = itm_flags.astype(jnp.float32)
    count_all, first_all, second_all = (
        one_axis_at_a_time(jnp.sum(money_all, axis=1), PATH),
        one_axis_at_a_time(jnp.sum(money_all[:, None, :] * states, axis=2), PATH),
        one_axis_at_a_time(jnp.sum(money_all[:, None, :] * states * states, axis=2), PATH),
    )
    mean_all = first_all / count_all[:, None]
    scale_all = jnp.sqrt(second_all / count_all[:, None] - mean_all * mean_all + 1e-05)
    local_list = []
    for date_step in range(date_count):
        scaled = (states[date_step] - mean_all[date_step][:, None]) / scale_all[date_step][:, None]
        local_list.append(gram_only(basis_of(scaled, pair_left, pair_right), money_all[date_step]))
    gram_stack = lax.psum(jnp.stack(local_list, axis=0), PATH)
    chol_list = [
        jnp.linalg.cholesky(system_of(gram_stack[date_step], count_all[date_step]))
        for date_step in range(date_count)
    ]
    for date_step in range(date_count - 1, -1, -1):
        factors = states[date_step]
        exercise, discount = swap_terms(factors, strike[0])
        value_now = value_now * discount
        money_flags = money_all[date_step]
        scaled = (factors - mean_all[date_step][:, None]) / scale_all[date_step][:, None]
        basis_rows = basis_of(scaled, pair_left, pair_right)
        rhs_local = jnp.dot(
            basis_rows * money_flags,
            value_now,
            precision=highest,
            preferred_element_type=jnp.float32,
        )
        rhs_total = over_copies(rhs_local, PATH)
        coef_vector = jax.scipy.linalg.cho_solve(
            (chol_list[date_step], True), rhs_total / count_all[date_step]
        )
        continuation = jnp.dot(
            coef_vector, basis_rows, precision=highest, preferred_element_type=jnp.float32
        )
        open_date = (date_index <= date_step).astype(jnp.float32)
        weights = jax.nn.sigmoid((exercise - continuation) / temper_scale) * money_flags * open_date
        value_now = value_now + weights * (exercise - value_now)
        coef_list.append(coef_vector)
    book_sum = one_axis_at_a_time(jnp.sum(value_now), PATH)
    book_price = jnp.reshape(book_sum / total_paths, (1,))
    return (value_now, book_price, jnp.stack(coef_list[::-1], axis=0))


def solution(mesh):
    split = Mesh(mesh.devices.reshape(mesh.shape["book"], 4, 4), ("book", "path_0", "path_1"))
    return jax.shard_map(
        shards,
        mesh=split,
        in_specs=(
            P(None, None, BOOK_PATH),
            P(None, BOOK_PATH),
            P(BOOK_PATH),
            P("book"),
            P(BOOK_PATH),
        ),
        out_specs=(P(BOOK_PATH), P("book"), P("book", None)),
        check_vma=False,
    )
```

profile of v0, /device:TPU:0, one launch (start us, length us, event | category | flops | bytes accessed | tf_op | source)
XLA Modules:
  0.0 1114.3 jit_solution(1723377565558352581)
XLA Ops:
  11.3 18.4 %all-reduce.4 = (f32[10,20]{1,0:T(8,128)S(1)}, f32[10]{0:T(128)S(1)}, f32[10,20]{1,0:T(8,128)S(1)}) all-reduce(f32[10,20]{1,0:T(8,128)S(1)} %get-tuple-element.80, f32[10]{0:T(128)S(1)} %convert_reduce_fusion, f32[10,20]{1,0:T(8,128)S(1)} %get-tuple-element.79), channel_id=1, replica_groups=mesh['book'=8,'path_0'=4,'path_1'=4] {'path_0'}, use_global_device_ids=true, to_apply=%region_9.0 | all-reduce | flops 410 | bytes 3280 | tf_op jit(solution)/shard_map/psum | solution.py:17
  29.7 17.0 %all-reduce.3 = (f32[10,20]{1,0:T(8,128)S(1)}, f32[10]{0:T(128)S(1)}, f32[10,20]{1,0:T(8,128)S(1)}) all-reduce(f32[10,20]{1,0:T(8,128)S(1)} %get-tuple-element.84, f32[10]{0:T(128)S(1)} %get-tuple-element.85, f32[10,20]{1,0:T(8,128)S(1)} %get-tuple-element.86), channel_id=1, replica_groups=mesh['book'=8,'path_0'=4,'path_1'=4] {'path_1'}, use_global_device_ids=true, to_apply=%region_10.11 | all-reduce | flops 410 | bytes 3280 | tf_op jit(solution)/shard_map/psum | solution.py:17
  184.8 69.2 %all-reduce.7.cloned.1.call-done = f32[10,231,231]{1,2,0:T(8,128)} async-done(((f32[10,231,231]{1,2,0:T(8,128)}), f32[10,231,231]{1,2,0:T(8,128)}) %all-reduce.7.cloned.1.call-update) | async-done | bytes 2134456 | tf_op jit(solution)/shard_map/psum | solution.py:78
  257.5 11.7 %cholesky.504 = f32[128,128]{1,0:T(8,128)S(1)} custom-call(f32[128,128]{1,0:T(8,128)S(1)} %cholesky.880), custom_call_target="Cholesky" | custom-call | tf_op jit(solution)/shard_map/jit(cholesky)/cholesky | solution.py:80
  269.9 9.8 custom-call.31
  280.2 9.4 cholesky.524
  292.9 8.2 select_add_fusion
  304.6 12.1 %cholesky.846 = f32[128,128]{1,0:T(8,128)S(1)} custom-call(f32[128,128]{1,0:T(8,128)S(1)} %cholesky.907), custom_call_target="Cholesky" | custom-call | tf_op jit(solution)/shard_map/jit(cholesky)/cholesky | solution.py:80
  318.1 9.8 custom-call.49
  330.7 9.4 cholesky.866
  348.6 12.7 %cholesky.808 = f32[128,128]{1,0:T(8,128)S(1)} custom-call(f32[128,128]{1,0:T(8,128)} %cholesky.904), custom_call_target="Cholesky" | custom-call | tf_op jit(solution)/shard_map/jit(cholesky)/cholesky | solution.py:80
  363.2 10.6 custom-call.47
  377.2 10.2 cholesky.828
  396.5 12.5 %cholesky.770 = f32[128,128]{1,0:T(8,128)S(1)} custom-call(f32[128,128]{1,0:T(8,128)} %cholesky.901), custom_call_target="Cholesky" | custom-call | tf_op jit(solution)/shard_map/jit(cholesky)/cholesky | solution.py:80
  411.1 10.6 custom-call.45
  425.3 10.2 cholesky.790
  442.9 11.7 %cholesky.732 = f32[128,128]{1,0:T(8,128)S(1)} custom-call(f32[128,128]{1,0:T(8,128)S(1)} %cholesky.898), custom_call_target="Cholesky" | custom-call | tf_op jit(solution)/shard_map/jit(cholesky)/cholesky | solution.py:80
  456.0 9.8 custom-call.43
  468.6 9.4 cholesky.752
  484.1 11.7 %cholesky.694 = f32[128,128]{1,0:T(8,128)S(1)} custom-call(f32[128,128]{1,0:T(8,128)S(1)} %cholesky.895), custom_call_target="Cholesky" | custom-call | tf_op jit(solution)/shard_map/jit(cholesky)/cholesky | solution.py:80
  497.2 9.8 custom-call.41
  509.8 9.4 cholesky.714
  523.6 11.9 %cholesky.656 = f32[128,128]{1,0:T(8,128)S(1)} custom-call(f32[128,128]{1,0:T(8,128)S(1)} %cholesky.892), custom_call_target="Cholesky" | custom-call | tf_op jit(solution)/shard_map/jit(cholesky)/cholesky | solution.py:80
  536.9 9.8 custom-call.39
  547.8 9.4 cholesky.676
  561.8 11.7 %cholesky.618 = f32[128,128]{1,0:T(8,128)S(1)} custom-call(f32[128,128]{1,0:T(8,128)S(1)} %cholesky.889), custom_call_target="Cholesky" | custom-call | tf_op jit(solution)/shard_map/jit(cholesky)/cholesky | solution.py:80
  574.8 10.2 custom-call.37
  586.2 9.4 cholesky.638
  600.0 11.7 %cholesky.580 = f32[128,128]{1,0:T(8,128)S(1)} custom-call(f32[128,128]{1,0:T(8,128)S(1)} %cholesky.886), custom_call_target="Cholesky" | custom-call | tf_op jit(solution)/shard_map/jit(cholesky)/cholesky | solution.py:80
  613.1 9.8 custom-call.35
  624.0 9.6 cholesky.600
  638.1 11.7 %cholesky.542 = f32[128,128]{1,0:T(8,128)S(1)} custom-call(f32[128,128]{1,0:T(8,128)S(1)} %cholesky.883), custom_call_target="Cholesky" | custom-call | tf_op jit(solution)/shard_map/jit(cholesky)/cholesky | solution.py:80
  651.2 9.8 custom-call.33
  662.1 9.4 cholesky.562
  676.6 19.7 %custom-call.32 = f32[2,128,128]{1,2,0:T(8,128)S(1)} custom-call(f32[2,128,128]{2,1,0:T(8,128)S(1)} %pad_maximum_fusion.10), custom_call_target="InvertDiagBlocksLowerTriangular" | custom-call | tf_op jit(solution)/shard_map/jit(_cho_solve)/triangular_solve | solution.py:97
  719.7 21.1 %custom-call.50 = f32[2,128,128]{1,2,0:T(8,128)} custom-call(f32[2,128,128]{2,1,0:T(8,128)} %pad_maximum_fusion.19), custom_call_target="InvertDiagBlocksLowerTriangular" | custom-call | tf_op jit(solution)/shard_map/jit(_cho_solve)/triangular_solve | solution.py:97
  740.8 21.1 %custom-call.36 = f32[2,128,128]{1,2,0:T(8,128)} custom-call(f32[2,128,128]{2,1,0:T(8,128)} %pad_maximum_fusion.12), custom_call_target="InvertDiagBlocksLowerTriangular" | custom-call | tf_op jit(solution)/shard_map/jit(_cho_solve)/triangular_solve | solution.py:97
  761.9 21.1 %custom-call.38 = f32[2,128,128]{1,2,0:T(8,128)} custom-call(f32[2,128,128]{2,1,0:T(8,128)} %pad_maximum_fusion.13), custom_call_target="InvertDiagBlocksLowerTriangular" | custom-call | tf_op jit(solution)/shard_map/jit(_cho_solve)/triangular_solve | solution.py:97
  783.0 21.1 %custom-call.40 = f32[2,128,128]{1,2,0:T(8,128)} custom-call(f32[2,128,128]{2,1,0:T(8,128)} %pad_maximum_fusion.14), custom_call_target="InvertDiagBlocksLowerTriangular" | custom-call | tf_op jit(solution)/shard_map/jit(_cho_solve)/triangular_solve | solution.py:97
  804.1 21.1 %custom-call.42 = f32[2,128,128]{1,2,0:T(8,128)} custom-call(f32[2,128,128]{2,1,0:T(8,128)} %pad_maximum_fusion.15), custom_call_target="InvertDiagBlocksLowerTriangular" | custom-call | tf_op jit(solution)/shard_map/jit(_cho_solve)/triangular_solve | solution.py:97
  825.2 21.3 %custom-call.44 = f32[2,128,128]{1,2,0:T(8,128)} custom-call(f32[2,128,128]{2,1,0:T(8,128)} %pad_maximum_fusion.16), custom_call_target="InvertDiagBlocksLowerTriangular" | custom-call | tf_op jit(solution)/shard_map/jit(_cho_solve)/triangular_solve | solution.py:97
  846.5 21.1 %custom-call.46 = f32[2,128,128]{1,2,0:T(8,128)} custom-call(f32[2,128,128]{2,1,0:T(8,128)} %pad_maximum_fusion.17), custom_call_target="InvertDiagBlocksLowerTriangular" | custom-call | tf_op jit(solution)/shard_map/jit(_cho_solve)/triangular_solve | solution.py:97
  867.6 21.1 %custom-call.48 = f32[2,128,128]{1,2,0:T(8,128)} custom-call(f32[2,128,128]{2,1,0:T(8,128)} %pad_maximum_fusion.18), custom_call_target="InvertDiagBlocksLowerTriangular" | custom-call | tf_op jit(solution)/shard_map/jit(_cho_solve)/triangular_solve | solution.py:97
  888.7 21.1 %custom-call.34 = f32[2,128,128]{1,2,0:T(8,128)} custom-call(f32[2,128,128]{2,1,0:T(8,128)} %pad_maximum_fusion.11), custom_call_target="InvertDiagBlocksLowerTriangular" | custom-call | tf_op jit(solution)/shard_map/jit(_cho_solve)/triangular_solve | solution.py:97
  924.3 7.5 all-to-all-start.2
  973.9 7.5 all-to-all-done.4
  1085.2 9.5 psum.70
  1094.7 9.5 psum.71
  (668 shorter events, 410.3 us)
Async XLA Ops:
  7.2 39.6 %copy-start.142 = (s32[210]{0:T(256)S(1)}, s32[210]{0:T(256)}, u32[]{:S(2)}) copy-start(s32[210]{0:T(256)} %constant.243) | copy-start | bytes 2524
  7.2 39.6 %copy-start.143 = (s32[210]{0:T(256)S(1)}, s32[210]{0:T(256)}, u32[]{:S(2)}) copy-start(s32[210]{0:T(256)} %constant.242) | copy-start | bytes 2524
  9.2 117.4 %copy-start.71 = (f32[1,2048]{1,0:T(1,128)}, f32[1,2048]{1,0:T(1,128)S(1)}, u32[]{:S(2)}) copy-start(f32[1,2048]{1,0:T(1,128)S(1)} %get-tuple-element.145) | copy-start | bytes 24580
  9.2 126.6 %copy-start.75 = (f32[1,2048]{1,0:T(1,128)}, f32[1,2048]{1,0:T(1,128)S(1)}, u32[]{:S(2)}) copy-start(f32[1,2048]{1,0:T(1,128)S(1)} %get-tuple-element.144) | copy-start | bytes 24580
  9.2 129.3 %copy-start.77 = (f32[1,2048]{1,0:T(1,128)}, f32[1,2048]{1,0:T(1,128)S(1)}, u32[]{:S(2)}) copy-start(f32[1,2048]{1,0:T(1,128)S(1)} %get-tuple-element.143) | copy-start | bytes 24580
  9.2 132.0 %copy-start.79 = (f32[1,2048]{1,0:T(1,128)}, f32[1,2048]{1,0:T(1,128)S(1)}, u32[]{:S(2)}) copy-start(f32[1,2048]{1,0:T(1,128)S(1)} %get-tuple-element.142) | copy-start | bytes 24580
  9.3 134.7 %copy-start.81 = (f32[1,2048]{1,0:T(1,128)}, f32[1,2048]{1,0:T(1,128)S(1)}, u32[]{:S(2)}) copy-start(f32[1,2048]{1,0:T(1,128)S(1)} %get-tuple-element.141) | copy-start | bytes 24580
  9.3 137.6 %copy-start.83 = (f32[1,2048]{1,0:T(1,128)}, f32[1,2048]{1,0:T(1,128)S(1)}, u32[]{:S(2)}) copy-start(f32[1,2048]{1,0:T(1,128)S(1)} %get-tuple-element.140) | copy-start | bytes 24580
  9.3 140.3 %copy-start.85 = (f32[1,2048]{1,0:T(1,128)}, f32[1,2048]{1,0:T(1,128)S(1)}, u32[]{:S(2)}) copy-start(f32[1,2048]{1,0:T(1,128)S(1)} %get-tuple-element.139) | copy-start | bytes 24580
  9.3 143.0 %copy-start.88 = (f32[1,2048]{1,0:T(1,128)}, f32[1,2048]{1,0:T(1,128)S(1)}, u32[]{:S(2)}) copy-start(f32[1,2048]{1,0:T(1,128)S(1)} %get-tuple-element.138) | copy-start | bytes 24580
  9.3 145.7 %copy-start.90 = (f32[1,2048]{1,0:T(1,128)}, f32[1,2048]{1,0:T(1,128)S(1)}, u32[]{:S(2)}) copy-start(f32[1,2048]{1,0:T(1,128)S(1)} %get-tuple-element.137) | copy-start | bytes 24580
  9.3 148.4 %copy-start.96 = (f32[1,2048]{1,0:T(1,128)}, f32[1,2048]{1,0:T(1,128)S(1)}, u32[]{:S(2)}) copy-start(f32[1,2048]{1,0:T(1,128)S(1)} %get-tuple-element.146) | copy-start | bytes 24580
  60.6 97.1 %copy-start.127 = (f32[1,2048]{1,0:T(1,128)}, f32[1,2048]{1,0:T(1,128)S(1)}, u32[]{:S(2)}) copy-start(f32[1,2048]{1,0:T(1,128)S(1)} %broadcast.242) | copy-start | bytes 24580
  62.9 121.1 %all-to-all-start = ((f32[16,1,231]{2,1,0:T(1,128)}), f32[16,1,231]{2,1,0:T(1,128)S(1)}, u32[]{:S(2)}, u32[]{:S(2)}) async-start(f32[16,1,231]{2,1,0:T(1,128)} %broadcast_in_dim.208), calls=%async_computation | async-start | bytes 32768 | tf_op jit(solution)/shard_map/all_to_all | solution.py:23
  66.7 187.3 %all-reduce.7.cloned.1.call-start = ((), (), s32[]{:S(2)}) async-start(), calls=%async_computation.10 | async-start | bytes 4751360 | tf_op jit(solution)/shard_map/psum | solution.py:78
  115.8 36.5 %copy-start.30 = (f32[210,2048]{1,0:T(8,128)}, f32[210,2048]{1,0:T(8,128)S(1)}, u32[]{:S(2)}) copy-start(f32[210,2048]{1,0:T(8,128)S(1)} %mul.603) | copy-start | bytes 5160964
  118.4 25.6 %copy-start.24 = (f32[210,2048]{1,0:T(8,128)}, f32[210,2048]{1,0:T(8,128)S(1)}, u32[]{:S(2)}) copy-start(f32[210,2048]{1,0:T(8,128)S(1)} %mul.591) | copy-start | bytes 5160964
  132.9 22.1 %copy-start.32 = (f32[210,2048]{1,0:T(8,128)}, f32[210,2048]{1,0:T(8,128)S(1)}, u32[]{:S(2)}) copy-start(f32[210,2048]{1,0:T(8,128)S(1)} %mul.607) | copy-start | bytes 5160964
  634.2 42.3 %copy-start.52 = (f32[128,25]{1,0:T(8,128)S(1)}, f32[128,25]{1,0:T(8,128)}, u32[]{:S(2)}) copy-start(f32[128,25]{1,0:T(8,128)} %pad_convert_fusion) | copy-start | bytes 38404
  634.2 42.3 %copy-start.61 = (f32[103,103]{1,0:T(8,128)S(1)}, f32[103,103]{1,0:T(8,128)}, u32[]{:S(2)}) copy-start(f32[103,103]{1,0:T(8,128)} %triangular_solve.700) | copy-start | bytes 127312
  636.2 40.4 %copy-start.60 = (f32[1,128,128]{2,1,0:T(8,128)S(1)}, f32[1,128,128]{2,1,0:T(8,128)}, u32[]{:S(2)}) copy-start(f32[1,128,128]{2,1,0:T(8,128)} %slice_bitcast_fusion.19) | copy-start | bytes 196612
  637.9 61.2 %copy-start.128 = (f32[1,2048]{1,0:T(1,128)S(1)}, f32[1,2048]{1,0:T(1,128)}, u32[]{:S(2)}) copy-start(f32[1,2048]{1,0:T(1,128)} %copy-done.127) | copy-start | bytes 24580
  672.8 29.0 %copy-start.46 = (s32[2048]{0:T(1024)S(1)}, s32[2048]{0:T(1024)}, u32[]{:S(2)}) copy-start(s32[2048]{0:T(1024)} %param.54) | copy-start | bytes 24580
  672.8 29.0 %copy-start.97 = (f32[1,2048]{1,0:T(1,128)S(1)}, f32[1,2048]{1,0:T(1,128)}, u32[]{:S(2)}) copy-start(f32[1,2048]{1,0:T(1,128)} %copy-done.96) | copy-start | bytes 24580
  672.8 29.0 %copy-start.101 = (f32[2048]{0:T(1024)S(1)}, f32[2048]{0:T(1024)}, u32[]{:S(2)}) copy-start(f32[2048]{0:T(1024)} %copy-done.100) | copy-start | bytes 24580
  672.8 29.1 %copy-start.118 = (f32[1,2048]{1,0:T(1,128)S(1)}, f32[1,2048]{1,0:T(1,128)}, u32[]{:S(2)}) copy-start(f32[1,2048]{1,0:T(1,128)} %get-tuple-element.135) | copy-start | bytes 24580
  672.8 29.1 %copy-start.121 = (f32[1,2048]{1,0:T(1,128)S(1)}, f32[1,2048]{1,0:T(1,128)}, u32[]{:S(2)}) copy-start(f32[1,2048]{1,0:T(1,128)} %get-tuple-element.134) | copy-start | bytes 24580
  674.2 27.7 %copy-start.91 = (f32[1,2048]{1,0:T(1,128)S(1)}, f32[1,2048]{1,0:T(1,128)}, u32[]{:S(2)}) copy-start(f32[1,2048]{1,0:T(1,128)} %copy-done.90) | copy-start | bytes 24580
  704.3 205.5 %all-to-all-start.1 = ((f32[16,1,231]{2,1,0:T(1,128)}), f32[16,1,231]{2,1,0:T(1,128)}, u32[]{:S(2)}, u32[]{:S(2)}) async-start(f32[16,1,231]{2,1,0:T(1,128)} %broadcast_in_dim.211), calls=%async_computation.1 | async-start | bytes 32768 | tf_op jit(solution)/shard_map/all_to_all | solution.py:23
  713.0 208.9 %copy-start.31 = (f32[210,2048]{1,0:T(8,128)S(1)}, f32[210,2048]{1,0:T(8,128)}, u32[]{:S(2)}) copy-start(f32[210,2048]{1,0:T(8,128)} %copy-done.30) | copy-start | bytes 5160964
  713.0 208.9 %copy-start.89 = (f32[1,2048]{1,0:T(1,128)S(1)}, f32[1,2048]{1,0:T(1,128)}, u32[]{:S(2)}) copy-start(f32[1,2048]{1,0:T(1,128)} %copy-done.88) | copy-start | bytes 24580
  923.6 24.9 %copy-start.102 = (f32[2048]{0:T(1024)S(1)}, f32[2048]{0:T(1024)}, u32[]{:S(2)}) copy-start(f32[2048]{0:T(1024)} %reduce_sum.223) | copy-start | bytes 24580
  923.6 24.9 %copy-start.116 = (f32[1,2048]{1,0:T(1,128)S(1)}, f32[1,2048]{1,0:T(1,128)}, u32[]{:S(2)}) copy-start(f32[1,2048]{1,0:T(1,128)} %get-tuple-element.130) | copy-start | bytes 24580
  923.7 24.9 %copy-start.117 = (f32[1,2048]{1,0:T(1,128)S(1)}, f32[1,2048]{1,0:T(1,128)}, u32[]{:S(2)}) copy-start(f32[1,2048]{1,0:T(1,128)} %get-tuple-element.131) | copy-start | bytes 24580
  923.7 24.9 %copy-start.125 = (f32[2048]{0:T(1024)S(1)}, f32[2048]{0:T(1024)}, u32[]{:S(2)}) copy-start(f32[2048]{0:T(1024)} %copy-done.124) | copy-start | bytes 24580
  923.7 24.9 %copy-start.29 = (f32[210,2048]{1,0:T(8,128)S(1)}, f32[210,2048]{1,0:T(8,128)}, u32[]{:S(2)}) copy-start(f32[210,2048]{1,0:T(8,128)} %copy-done.28) | copy-start | bytes 5160964
  923.7 24.9 %copy-start.86 = (f32[1,2048]{1,0:T(1,128)S(1)}, f32[1,2048]{1,0:T(1,128)}, u32[]{:S(2)}) copy-start(f32[1,2048]{1,0:T(1,128)} %copy-done.85) | copy-start | bytes 24580
  923.7 24.9 %copy-start.130 = (f32[1,2048]{1,0:T(1,128)S(1)}, f32[1,2048]{1,0:T(1,128)}, u32[]{:S(2)}) copy-start(f32[1,2048]{1,0:T(1,128)} %copy-done.127) | copy-start | bytes 24580
  924.3 14.9 %all-to-all-start.2 = ((f32[16,1,231]{2,1,0:T(1,128)}), f32[16,1,231]{2,1,0:T(1,128)S(1)}, u32[]{:S(2)}, u32[]{:S(2)}) async-start(f32[16,1,231]{2,1,0:T(1,128)} %broadcast_in_dim.214), calls=%async_computation.2 | async-start | bytes 32768 | tf_op jit(solution)/shard_map/all_to_all | solution.py:23
  951.0 11.0 all-to-all-start.3
  970.4 11.0 all-to-all-start.4
  990.0 11.4 %all-to-all-start.5 = ((f32[16,1,231]{2,1,0:T(1,128)}), f32[16,1,231]{2,1,0:T(1,128)S(1)}, u32[]{:S(2)}, u32[]{:S(2)}) async-start(f32[16,1,231]{2,1,0:T(1,128)} %broadcast_in_dim.223), calls=%async_computation.5 | async-start | bytes 32768 | tf_op jit(solution)/shard_map/all_to_all | solution.py:23
  1009.8 11.0 all-to-all-start.6
  1029.3 11.0 all-to-all-start.7
  1048.7 11.2 %all-to-all-start.8 = ((f32[16,1,231]{2,1,0:T(1,128)}), f32[16,1,231]{2,1,0:T(1,128)S(1)}, u32[]{:S(2)}, u32[]{:S(2)}) async-start(f32[16,1,231]{2,1,0:T(1,128)} %broadcast_in_dim.232), calls=%async_computation.8 | async-start | bytes 32768 | tf_op jit(solution)/shard_map/all_to_all | solution.py:23
  1067.7 37.1 %copy-start.136 = (f32[1,231]{1,0:T(1,128)S(1)}, f32[1,231]{1,0:T(1,128)}, u32[]{:S(2)}) copy-start(f32[1,231]{1,0:T(1,128)} %fusion.420) | copy-start | bytes 2776
  1067.8 37.1 %copy-start.137 = (f32[1,231]{1,0:T(1,128)S(1)}, f32[1,231]{1,0:T(1,128)}, u32[]{:S(2)}) copy-start(f32[1,231]{1,0:T(1,128)} %fusion.419) | copy-start | bytes 2776
  1068.4 11.0 all-to-all-start.9
  (107 other events, 1008.8 us)
Sparse Core Ops, SparseCore 0:
  160.6 93.2 all-reduce.6
where the time goes:
time: 1120 us; the launch traced here: 1110 us
  other arithmetic  630 us (56%)
  waiting for transfers between devices  127 us (11%)
  matrix products  123 us (11%)
  local copies, waits for them, and re-layouts  106 us (9%)
  blocking collectives  54.3 us (5%)
  starting transfers between devices  41.8 us (4%)
  between operations  31.9 us (3%)
    another operation x70, other arithmetic, shards(): jnp.linalg.cholesky(system_of(gram_stack[date_step], count_all[date_step]))  336 us
    another operation x34, other arithmetic, shards(): jax.scipy.linalg.cho_solve((chol_list[date_step], True), rhs_total / coun...  229 us
    psum x1, waiting for transfers between devices, shards(): gram_stack = lax.psum(jnp.stack(local_list, axis=0), PATH)  69.2 us
    all_to_all x10, waiting for transfers between devices, sent_to_all(): lax.all_to_all(jnp.broadcast_to(shard[None], (length, *shard.shape)), axi...  58 us
    psum x4, blocking collectives, one_axis_at_a_time(): shard = lax.psum(shard, axis)  54.3 us
    all_to_all x10, starting transfers between devices, sent_to_all(): lax.all_to_all(jnp.broadcast_to(shard[None], (length, *shard.shape)), axi...  41.5 us
    another operation x60, matrix products, shards(): jax.scipy.linalg.cho_solve((chol_list[date_step], True), rhs_total / coun...  33.7 us
    dot_general x10, matrix products, gram_only(): lax.dot_general(weighted, basis_rows, (((1,), (1,)), ((), ())), precision...  27.3 us
  transfers between devices with their start and end apart: 11, of which 9 were waited for; matrix products, arithmetic and copies ran while one was open for 27% of the time, Pallas kernels for 0%

commit v1 on v0

--- a/solution.py
+++ b/solution.py
@@ -1,3 +1,4 @@
+import functools
 import jax
 import jax.numpy as jnp
 import numpy as np
@@ -10,6 +11,15 @@
 ridge_weight = 0.05
 temper_scale = 0.5
 highest = lax.Precision.HIGHEST
+
+
+def start_boxes(z_in, chip_axis, axis_name):
+    finding = lax.psum(z_in, axis_name=chip_axis)
+    field_out = lax.psum(finding, axis_name=axis_name)
+    return field_out
+
+
+feed_sheet = functools.partial(start_boxes, chip_axis="path_0", axis_name="path_1")
 
 
 def one_axis_at_a_time(shard, axes):
@@ -75,7 +85,7 @@
     for date_step in range(date_count):
         scaled = (states[date_step] - mean_all[date_step][:, None]) / scale_all[date_step][:, None]
         local_list.append(gram_only(basis_of(scaled, pair_left, pair_right), money_all[date_step]))
-    gram_stack = lax.psum(jnp.stack(local_list, axis=0), PATH)
+    gram_stack = feed_sheet(jnp.stack(local_list, axis=0))
     chol_list = [
         jnp.linalg.cholesky(system_of(gram_stack[date_step], count_all[date_step]))
         for date_step in range(date_count)

time: 1120 us -> 1180 us (1.054)
  waiting for transfers between devices: 127 us -> 167 us
    psum x1 -> x2, waiting for transfers between devices: 69.2 us -> 107 us  [the longest x1 55.9 us: start_boxes(): finding = lax.psum(z_in, axis_name=chip_axis)]
    dot_general x10, matrix products: 16.6 us -> 28.5 us  [shards(): jnp.dot(basis_rows * money_flags, value_now, precision=highest, preferred...]
    unnamed x288 -> x218, local copies, waits for them, and re-layouts: 22.9 us -> 24.1 us
  transfers between devices with their start and end apart: 11 -> 12, of which waited for: 9 -> 10; matrix products, arithmetic and copies ran while one was open for 27% -> 26% of each run, Pallas kernels for 0% -> 0%
where the time goes in v1:
time: 1180 us; the launch traced here: 1170 us
  other arithmetic  629 us (53%)
  waiting for transfers between devices  167 us (14%)
  matrix products  131 us (11%)
  local copies, waits for them, and re-layouts  109 us (9%)
  blocking collectives  54.3 us (5%)
  starting transfers between devices  42.8 us (4%)
  between operations  31.5 us (3%)
    another operation x70, other arithmetic, shards(): jnp.linalg.cholesky(system_of(gram_stack[date_step], count_all[date_step]))  336 us
    another operation x34, other arithmetic, shards(): jax.scipy.linalg.cho_solve((chol_list[date_step], True), rhs_total / coun...  231 us
    all_to_all x10, waiting for transfers between devices, sent_to_all(): lax.all_to_all(jnp.broadcast_to(shard[None], (length, *shard.shape)), axi...  60.1 us
    psum x1, waiting for transfers between devices, start_boxes(): finding = lax.psum(z_in, axis_name=chip_axis)  55.9 us
    psum x4, blocking collectives, one_axis_at_a_time(): shard = lax.psum(shard, axis)  54.3 us
    psum x1, waiting for transfers between devices, start_boxes(): field_out = lax.psum(finding, axis_name=axis_name)  51 us
    all_to_all x10, starting transfers between devices, sent_to_all(): lax.all_to_all(jnp.broadcast_to(shard[None], (length, *shard.shape)), axi...  42.2 us
    dot_general x10, matrix products, shards(): jnp.dot(basis_rows * money_flags, value_now, precision=highest, preferred...  28.5 us
  transfers between devices with their start and end apart: 12, of which 10 were waited for; matrix products, arithmetic and copies ran while one was open for 26% of the time, Pallas kernels for 0%

profile of v1, /device:TPU:0, one launch (start us, length us, event | category | flops | bytes accessed | tf_op | source)
XLA Modules:
  0.0 1165.6 jit_solution(866275226232868939)
XLA Ops:
  11.3 18.4 %all-reduce.4 = (f32[10,20]{1,0:T(8,128)S(1)}, f32[10]{0:T(128)S(1)}, f32[10,20]{1,0:T(8,128)S(1)}) all-reduce(f32[10,20]{1,0:T(8,128)S(1)} %get-tuple-element.80, f32[10]{0:T(128)S(1)} %convert_reduce_fusion, f32[10,20]{1,0:T(8,128)S(1)} %get-tuple-element.79), channel_id=1, replica_groups=mesh['book'=8,'path_0'=4,'path_1'=4] {'path_0'}, use_global_device_ids=true, to_apply=%region_9.0 | all-reduce | flops 410 | bytes 3280 | tf_op jit(solution)/shard_map/psum | solution.py:27
  29.7 17.0 %all-reduce.3 = (f32[10,20]{1,0:T(8,128)S(1)}, f32[10]{0:T(128)S(1)}, f32[10,20]{1,0:T(8,128)S(1)}) all-reduce(f32[10,20]{1,0:T(8,128)S(1)} %get-tuple-element.84, f32[10]{0:T(128)S(1)} %get-tuple-element.85, f32[10,20]{1,0:T(8,128)S(1)} %get-tuple-element.86), channel_id=1, replica_groups=mesh['book'=8,'path_0'=4,'path_1'=4] {'path_1'}, use_global_device_ids=true, to_apply=%region_10.0 | all-reduce | flops 410 | bytes 3280 | tf_op jit(solution)/shard_map/psum | solution.py:27
  170.0 55.9 %all-reduce.8.cloned.1.call-done = f32[10,231,231]{1,2,0:T(8,128)} async-done(((f32[10,231,231]{1,2,0:T(8,128)}), f32[10,231,231]{1,2,0:T(8,128)}) %all-reduce.8.cloned.1.call-update) | async-done | bytes 2134456 | tf_op jit(solution)/shard_map/psum | solution.py:17
  240.2 51.0 %all-reduce.10.cloned.1.call-done = f32[10,231,231]{1,2,0:T(8,128)} async-done(((f32[10,231,231]{1,2,0:T(8,128)}), f32[10,231,231]{1,2,0:T(8,128)}) %all-reduce.10.cloned.1.call-update) | async-done | bytes 2134456 | tf_op jit(solution)/shard_map/psum | solution.py:18
  294.7 11.7 %cholesky.504 = f32[128,128]{1,0:T(8,128)S(1)} custom-call(f32[128,128]{1,0:T(8,128)S(1)} %cholesky.880), custom_call_target="Cholesky" | custom-call | tf_op jit(solution)/shard_map/jit(cholesky)/cholesky | solution.py:90
  307.1 9.8 custom-call.31
  317.4 9.4 cholesky.524
  330.1 8.3 select_add_fusion
  342.0 12.1 %cholesky.846 = f32[128,128]{1,0:T(8,128)S(1)} custom-call(f32[128,128]{1,0:T(8,128)S(1)} %cholesky.907), custom_call_target="Cholesky" | custom-call | tf_op jit(solution)/shard_map/jit(cholesky)/cholesky | solution.py:90
  355.5 9.8 custom-call.49
  368.0 9.4 cholesky.866
  385.9 12.7 %cholesky.808 = f32[128,128]{1,0:T(8,128)S(1)} custom-call(f32[128,128]{1,0:T(8,128)} %cholesky.904), custom_call_target="Cholesky" | custom-call | tf_op jit(solution)/shard_map/jit(cholesky)/cholesky | solution.py:90
  400.6 10.6 custom-call.47
  414.6 10.2 cholesky.828
  433.8 12.5 %cholesky.770 = f32[128,128]{1,0:T(8,128)S(1)} custom-call(f32[128,128]{1,0:T(8,128)} %cholesky.901), custom_call_target="Cholesky" | custom-call | tf_op jit(solution)/shard_map/jit(cholesky)/cholesky | solution.py:90
  448.4 10.8 custom-call.45
  462.5 10.2 cholesky.790
  480.2 11.7 %cholesky.732 = f32[128,128]{1,0:T(8,128)S(1)} custom-call(f32[128,128]{1,0:T(8,128)S(1)} %cholesky.898), custom_call_target="Cholesky" | custom-call | tf_op jit(solution)/shard_map/jit(cholesky)/cholesky | solution.py:90
  493.2 9.8 custom-call.43
  505.8 9.8 cholesky.752
  521.3 11.7 %cholesky.694 = f32[128,128]{1,0:T(8,128)S(1)} custom-call(f32[128,128]{1,0:T(8,128)S(1)} %cholesky.895), custom_call_target="Cholesky" | custom-call | tf_op jit(solution)/shard_map/jit(cholesky)/cholesky | solution.py:90
  534.4 9.8 custom-call.41
  547.0 9.4 cholesky.714
  562.1 11.9 %cholesky.656 = f32[128,128]{1,0:T(8,128)S(1)} custom-call(f32[128,128]{1,0:T(8,128)S(1)} %cholesky.892), custom_call_target="Cholesky" | custom-call | tf_op jit(solution)/shard_map/jit(cholesky)/cholesky | solution.py:90
  575.3 9.8 custom-call.39
  587.9 9.4 cholesky.676
  602.9 11.7 %cholesky.618 = f32[128,128]{1,0:T(8,128)S(1)} custom-call(f32[128,128]{1,0:T(8,128)S(1)} %cholesky.889), custom_call_target="Cholesky" | custom-call | tf_op jit(solution)/shard_map/jit(cholesky)/cholesky | solution.py:90
  616.0 10.2 custom-call.37
  629.0 9.4 cholesky.638
  644.0 11.7 %cholesky.580 = f32[128,128]{1,0:T(8,128)S(1)} custom-call(f32[128,128]{1,0:T(8,128)S(1)} %cholesky.886), custom_call_target="Cholesky" | custom-call | tf_op jit(solution)/shard_map/jit(cholesky)/cholesky | solution.py:90
  657.1 9.8 custom-call.35
  669.7 9.6 cholesky.600
  685.0 11.7 %cholesky.542 = f32[128,128]{1,0:T(8,128)S(1)} custom-call(f32[128,128]{1,0:T(8,128)S(1)} %cholesky.883), custom_call_target="Cholesky" | custom-call | tf_op jit(solution)/shard_map/jit(cholesky)/cholesky | solution.py:90
  698.0 9.8 custom-call.33
  710.6 9.4 cholesky.562
  726.5 20.5 %custom-call.32 = f32[2,128,128]{1,2,0:T(8,128)S(1)} custom-call(f32[2,128,128]{2,1,0:T(8,128)} %pad_maximum_fusion.10), custom_call_target="InvertDiagBlocksLowerTriangular" | custom-call | tf_op jit(solution)/shard_map/jit(_cho_solve)/triangular_solve | solution.py:107
  774.6 20.5 %custom-call.50 = f32[2,128,128]{1,2,0:T(8,128)S(1)} custom-call(f32[2,128,128]{2,1,0:T(8,128)} %pad_maximum_fusion.19), custom_call_target="InvertDiagBlocksLowerTriangular" | custom-call | tf_op jit(solution)/shard_map/jit(_cho_solve)/triangular_solve | solution.py:107
  795.1 20.3 %custom-call.36 = f32[2,128,128]{1,2,0:T(8,128)} custom-call(f32[2,128,128]{2,1,0:T(8,128)S(1)} %pad_maximum_fusion.12), custom_call_target="InvertDiagBlocksLowerTriangular" | custom-call | tf_op jit(solution)/shard_map/jit(_cho_solve)/triangular_solve | solution.py:107
  815.3 21.1 %custom-call.38 = f32[2,128,128]{1,2,0:T(8,128)} custom-call(f32[2,128,128]{2,1,0:T(8,128)} %pad_maximum_fusion.13), custom_call_target="InvertDiagBlocksLowerTriangular" | custom-call | tf_op jit(solution)/shard_map/jit(_cho_solve)/triangular_solve | solution.py:107
  836.4 21.1 %custom-call.40 = f32[2,128,128]{1,2,0:T(8,128)} custom-call(f32[2,128,128]{2,1,0:T(8,128)} %pad_maximum_fusion.14), custom_call_target="InvertDiagBlocksLowerTriangular" | custom-call | tf_op jit(solution)/shard_map/jit(_cho_solve)/triangular_solve | solution.py:107
  857.5 21.1 %custom-call.42 = f32[2,128,128]{1,2,0:T(8,128)} custom-call(f32[2,128,128]{2,1,0:T(8,128)} %pad_maximum_fusion.15), custom_call_target="InvertDiagBlocksLowerTriangular" | custom-call | tf_op jit(solution)/shard_map/jit(_cho_solve)/triangular_solve | solution.py:107
  878.6 20.4 %custom-call.44 = f32[2,128,128]{1,2,0:T(8,128)} custom-call(f32[2,128,128]{2,1,0:T(8,128)S(1)} %pad_maximum_fusion.16), custom_call_target="InvertDiagBlocksLowerTriangular" | custom-call | tf_op jit(solution)/shard_map/jit(_cho_solve)/triangular_solve | solution.py:107
  899.1 20.5 %custom-call.46 = f32[2,128,128]{1,2,0:T(8,128)S(1)} custom-call(f32[2,128,128]{2,1,0:T(8,128)} %pad_maximum_fusion.17), custom_call_target="InvertDiagBlocksLowerTriangular" | custom-call | tf_op jit(solution)/shard_map/jit(_cho_solve)/triangular_solve | solution.py:107
  919.5 20.5 %custom-call.48 = f32[2,128,128]{1,2,0:T(8,128)S(1)} custom-call(f32[2,128,128]{2,1,0:T(8,128)} %pad_maximum_fusion.18), custom_call_target="InvertDiagBlocksLowerTriangular" | custom-call | tf_op jit(solution)/shard_map/jit(_cho_solve)/triangular_solve | solution.py:107
  940.0 21.1 %custom-call.34 = f32[2,128,128]{1,2,0:T(8,128)} custom-call(f32[2,128,128]{2,1,0:T(8,128)} %pad_maximum_fusion.11), custom_call_target="InvertDiagBlocksLowerTriangular" | custom-call | tf_op jit(solution)/shard_map/jit(_cho_solve)/triangular_solve | solution.py:107
  981.1 7.6 all-to-all-done.2
  1136.5 9.5 psum.78
  1146.0 9.5 psum.79
  (601 shorter events, 433.9 us)
Async XLA Ops:
  7.2 39.6 %copy-start.107 = (s32[210]{0:T(256)S(1)}, s32[210]{0:T(256)}, u32[]{:S(2)}) copy-start(s32[210]{0:T(256)} %constant.243) | copy-start | bytes 2524
  7.2 39.6 %copy-start.108 = (s32[210]{0:T(256)S(1)}, s32[210]{0:T(256)}, u32[]{:S(2)}) copy-start(s32[210]{0:T(256)} %constant.242) | copy-start | bytes 2524
  9.2 117.4 %copy-start.51 = (f32[1,2048]{1,0:T(1,128)}, f32[1,2048]{1,0:T(1,128)S(1)}, u32[]{:S(2)}) copy-start(f32[1,2048]{1,0:T(1,128)S(1)} %get-tuple-element.145) | copy-start | bytes 24580
  9.2 126.5 %copy-start.55 = (f32[1,2048]{1,0:T(1,128)}, f32[1,2048]{1,0:T(1,128)S(1)}, u32[]{:S(2)}) copy-start(f32[1,2048]{1,0:T(1,128)S(1)} %get-tuple-element.144) | copy-start | bytes 24580
  9.2 129.3 %copy-start.57 = (f32[1,2048]{1,0:T(1,128)}, f32[1,2048]{1,0:T(1,128)S(1)}, u32[]{:S(2)}) copy-start(f32[1,2048]{1,0:T(1,128)S(1)} %get-tuple-element.143) | copy-start | bytes 24580
  9.2 132.0 %copy-start.59 = (f32[1,2048]{1,0:T(1,128)}, f32[1,2048]{1,0:T(1,128)S(1)}, u32[]{:S(2)}) copy-start(f32[1,2048]{1,0:T(1,128)S(1)} %get-tuple-element.142) | copy-start | bytes 24580
  9.3 134.7 %copy-start.61 = (f32[1,2048]{1,0:T(1,128)}, f32[1,2048]{1,0:T(1,128)S(1)}, u32[]{:S(2)}) copy-start(f32[1,2048]{1,0:T(1,128)S(1)} %get-tuple-element.141) | copy-start | bytes 24580
  9.3 137.6 %copy-start.63 = (f32[1,2048]{1,0:T(1,128)}, f32[1,2048]{1,0:T(1,128)S(1)}, u32[]{:S(2)}) copy-start(f32[1,2048]{1,0:T(1,128)S(1)} %get-tuple-element.140) | copy-start | bytes 24580
  9.3 140.3 %copy-start.65 = (f32[1,2048]{1,0:T(1,128)}, f32[1,2048]{1,0:T(1,128)S(1)}, u32[]{:S(2)}) copy-start(f32[1,2048]{1,0:T(1,128)S(1)} %get-tuple-element.139) | copy-start | bytes 24580
  9.3 143.0 %copy-start.67 = (f32[1,2048]{1,0:T(1,128)}, f32[1,2048]{1,0:T(1,128)S(1)}, u32[]{:S(2)}) copy-start(f32[1,2048]{1,0:T(1,128)S(1)} %get-tuple-element.138) | copy-start | bytes 24580
  9.3 145.7 %copy-start.70 = (f32[1,2048]{1,0:T(1,128)}, f32[1,2048]{1,0:T(1,128)S(1)}, u32[]{:S(2)}) copy-start(f32[1,2048]{1,0:T(1,128)S(1)} %get-tuple-element.137) | copy-start | bytes 24580
  9.3 148.4 %copy-start.74 = (f32[1,2048]{1,0:T(1,128)}, f32[1,2048]{1,0:T(1,128)S(1)}, u32[]{:S(2)}) copy-start(f32[1,2048]{1,0:T(1,128)S(1)} %get-tuple-element.146) | copy-start | bytes 24580
  60.6 97.1 %copy-start.101 = (f32[1,2048]{1,0:T(1,128)}, f32[1,2048]{1,0:T(1,128)S(1)}, u32[]{:S(2)}) copy-start(f32[1,2048]{1,0:T(1,128)S(1)} %broadcast.242) | copy-start | bytes 24580
  62.9 176.6 %all-to-all-start = ((f32[16,1,231]{2,1,0:T(1,128)}), f32[16,1,231]{2,1,0:T(1,128)S(1)}, u32[]{:S(2)}, u32[]{:S(2)}) async-start(f32[16,1,231]{2,1,0:T(1,128)} %broadcast_in_dim.208), calls=%async_computation | async-start | bytes 32768 | tf_op jit(solution)/shard_map/all_to_all | solution.py:33
  66.7 159.3 %all-reduce.8.cloned.1.call-start = ((), (), s32[]{:S(2)}) async-start(), calls=%async_computation.10 | async-start | bytes 4751360 | tf_op jit(solution)/shard_map/psum | solution.py:17
  115.7 36.6 %copy-start.23 = (f32[210,2048]{1,0:T(8,128)}, f32[210,2048]{1,0:T(8,128)S(1)}, u32[]{:S(2)}) copy-start(f32[210,2048]{1,0:T(8,128)S(1)} %mul.603) | copy-start | bytes 5160964
  118.4 25.6 %copy-start.20 = (f32[210,2048]{1,0:T(8,128)}, f32[210,2048]{1,0:T(8,128)S(1)}, u32[]{:S(2)}) copy-start(f32[210,2048]{1,0:T(8,128)S(1)} %mul.591) | copy-start | bytes 5160964
  121.0 20.2 %copy-start.19 = (f32[210,2048]{1,0:T(8,128)}, f32[210,2048]{1,0:T(8,128)S(1)}, u32[]{:S(2)}) copy-start(f32[210,2048]{1,0:T(8,128)S(1)} %mul.587) | copy-start | bytes 5160964
  132.8 22.2 %copy-start.24 = (f32[210,2048]{1,0:T(8,128)}, f32[210,2048]{1,0:T(8,128)S(1)}, u32[]{:S(2)}) copy-start(f32[210,2048]{1,0:T(8,128)S(1)} %mul.607) | copy-start | bytes 5160964
  160.5 130.7 %all-reduce.10.cloned.1.call-start = ((), (), s32[]{:S(2)}) async-start(), calls=%async_computation.11 | async-start | bytes 4751360 | tf_op jit(solution)/shard_map/psum | solution.py:18
  679.9 45.0 %copy-start.43 = (f32[128,25]{1,0:T(8,128)S(1)}, f32[128,25]{1,0:T(8,128)}, u32[]{:S(2)}) copy-start(f32[128,25]{1,0:T(8,128)} %pad_convert_fusion) | copy-start | bytes 38404
  684.1 65.7 %copy-start.102 = (f32[1,2048]{1,0:T(1,128)S(1)}, f32[1,2048]{1,0:T(1,128)}, u32[]{:S(2)}) copy-start(f32[1,2048]{1,0:T(1,128)} %copy-done.101) | copy-start | bytes 24580
  685.0 40.8 %copy-start.49 = (f32[1,128,128]{2,1,0:T(8,128)S(1)}, f32[1,128,128]{2,1,0:T(8,128)}, u32[]{:S(2)}) copy-start(f32[1,128,128]{2,1,0:T(8,128)} %slice_bitcast_fusion.19) | copy-start | bytes 196612
  721.3 31.2 %copy-start.33 = (s32[2048]{0:T(1024)S(1)}, s32[2048]{0:T(1024)}, u32[]{:S(2)}) copy-start(s32[2048]{0:T(1024)} %param.54) | copy-start | bytes 24580
  721.3 31.2 %copy-start.75 = (f32[1,2048]{1,0:T(1,128)S(1)}, f32[1,2048]{1,0:T(1,128)}, u32[]{:S(2)}) copy-start(f32[1,2048]{1,0:T(1,128)} %copy-done.74) | copy-start | bytes 24580
  721.3 31.2 %copy-start.79 = (f32[2048]{0:T(1024)S(1)}, f32[2048]{0:T(1024)}, u32[]{:S(2)}) copy-start(f32[2048]{0:T(1024)} %copy-done.78) | copy-start | bytes 24580
  721.3 31.2 %copy-start.81 = (f32[2048]{0:T(1024)S(1)}, f32[2048]{0:T(1024)}, u32[]{:S(2)}) copy-start(f32[2048]{0:T(1024)} %reduce_sum.216) | copy-start | bytes 24580
  721.3 31.2 %copy-start.95 = (f32[1,2048]{1,0:T(1,128)S(1)}, f32[1,2048]{1,0:T(1,128)}, u32[]{:S(2)}) copy-start(f32[1,2048]{1,0:T(1,128)} %get-tuple-element.135) | copy-start | bytes 24580
  721.3 31.2 %copy-start.98 = (f32[1,2048]{1,0:T(1,128)S(1)}, f32[1,2048]{1,0:T(1,128)}, u32[]{:S(2)}) copy-start(f32[1,2048]{1,0:T(1,128)} %get-tuple-element.134) | copy-start | bytes 24580
  722.7 29.9 %copy-start.71 = (f32[1,2048]{1,0:T(1,128)S(1)}, f32[1,2048]{1,0:T(1,128)}, u32[]{:S(2)}) copy-start(f32[1,2048]{1,0:T(1,128)} %copy-done.70) | copy-start | bytes 24580
  754.9 206.3 %all-to-all-start.1 = ((f32[16,1,231]{2,1,0:T(1,128)}), f32[16,1,231]{2,1,0:T(1,128)S(1)}, u32[]{:S(2)}, u32[]{:S(2)}) async-start(f32[16,1,231]{2,1,0:T(1,128)} %broadcast_in_dim.211), calls=%async_computation.1 | async-start | bytes 32768 | tf_op jit(solution)/shard_map/all_to_all | solution.py:33
  768.0 201.0 %copy-start.80 = (f32[2048]{0:T(1024)S(1)}, f32[2048]{0:T(1024)}, u32[]{:S(2)}) copy-start(f32[2048]{0:T(1024)} %reduce_sum.221) | copy-start | bytes 24580
  768.0 201.0 %copy-start.97 = (f32[1,2048]{1,0:T(1,128)S(1)}, f32[1,2048]{1,0:T(1,128)}, u32[]{:S(2)}) copy-start(f32[1,2048]{1,0:T(1,128)} %get-tuple-element.132) | copy-start | bytes 24580
  768.0 201.8 %copy-start.68 = (f32[1,2048]{1,0:T(1,128)S(1)}, f32[1,2048]{1,0:T(1,128)}, u32[]{:S(2)}) copy-start(f32[1,2048]{1,0:T(1,128)} %copy-done.67) | copy-start | bytes 24580
  969.0 20.4 %copy-start.48 = (f32[2,128,128]{1,2,0:T(8,128)S(1)}, f32[2,128,128]{1,2,0:T(8,128)}, u32[]{:S(2)}) copy-start(f32[2,128,128]{1,2,0:T(8,128)} %custom-call.36) | copy-start | bytes 393220
  969.0 21.5 %copy-start.103 = (f32[1,2048]{1,0:T(1,128)S(1)}, f32[1,2048]{1,0:T(1,128)}, u32[]{:S(2)}) copy-start(f32[1,2048]{1,0:T(1,128)} %copy-done.101) | copy-start | bytes 24580
  972.9 20.2 %copy-start.94 = (f32[1,2048]{1,0:T(1,128)S(1)}, f32[1,2048]{1,0:T(1,128)}, u32[]{:S(2)}) copy-start(f32[1,2048]{1,0:T(1,128)} %get-tuple-element.130) | copy-start | bytes 24580
  972.9 20.2 %copy-start.96 = (f32[1,2048]{1,0:T(1,128)S(1)}, f32[1,2048]{1,0:T(1,128)}, u32[]{:S(2)}) copy-start(f32[1,2048]{1,0:T(1,128)} %get-tuple-element.131) | copy-start | bytes 24580
  972.9 20.2 %copy-start.66 = (f32[1,2048]{1,0:T(1,128)S(1)}, f32[1,2048]{1,0:T(1,128)}, u32[]{:S(2)}) copy-start(f32[1,2048]{1,0:T(1,128)} %copy-done.65) | copy-start | bytes 24580
  973.6 15.1 %all-to-all-start.2 = ((f32[16,1,231]{2,1,0:T(1,128)}), f32[16,1,231]{2,1,0:T(1,128)S(1)}, u32[]{:S(2)}, u32[]{:S(2)}) async-start(f32[16,1,231]{2,1,0:T(1,128)} %broadcast_in_dim.214), calls=%async_computation.2 | async-start | bytes 32768 | tf_op jit(solution)/shard_map/all_to_all | solution.py:33
  997.0 11.0 all-to-all-start.3
  1016.3 11.0 all-to-all-start.4
  1035.6 11.4 all-to-all-start.5
  1055.3 11.0 all-to-all-start.6
  1076.3 11.0 all-to-all-start.7
  1097.2 11.2 all-to-all-start.8
  1117.7 38.5 %copy-start.105 = (f32[1,231]{1,0:T(1,128)S(1)}, f32[1,231]{1,0:T(1,128)}, u32[]{:S(2)}) copy-start(f32[1,231]{1,0:T(1,128)} %fusion.420) | copy-start | bytes 2776
  1118.3 11.0 all-to-all-start.9
  (73 other events, 621.9 us)
Sparse Core Ops, SparseCore 0:
  160.6 65.2 all-reduce.7
  228.3 62.8 all-reduce.9
